TPU v7x, 128 devices: a whole 4x4x4 slice. The times are simulated.
128 devices in a mesh: pipe: 2 (over x_lo), tensor: 4 (over x_hi, core), dp: 16 (over z, y).
Axes of the slice: x: 4 (x_hi: 2, x_lo: 2; x = x_hi * 2 + x_lo), y: 4, z: 4, core: 2. Of those that a mesh axis runs over, the one named last changes fastest.
Arguments:
- inputs: bfloat16 [2, 2048, 16384], P(None, 'dp', 'tensor'), may hold values from -6 to 6
- w_in: bfloat16 [2, 16384, 1024], P('pipe', ('tensor', 'dp')), may hold values from -0.046875 to 0.046875
- w_out: bfloat16 [2, 1024, 16384], P('pipe', None, ('tensor', 'dp')), may hold values from -0.1875 to 0.1875
- cotangent: bfloat16 [2, 2048, 16384], P(None, 'dp', 'tensor'), may hold values from -6 to 6
Outputs:
- update_in: float32 [2, 16384, 1024], P('pipe', ('tensor', 'dp'))
- update_out: float32 [2, 1024, 16384], P('pipe', None, ('tensor', 'dp'))
- grad_norm: float32 [], replicated
All inputs are finite; a program needn't handle non-finite values.
Results may differ from a plain program's by a relative error of at most 0.008.
Values may be sent and summed in bfloat16 or wider, within the bound.
A program may use at most 192 MiB of HBM per device.

v0:
```python
import jax
import jax.numpy as jnp
from jax import lax
from jax.sharding import Mesh
from jax.sharding import PartitionSpec as P

CLIP_NORM = 16384
DP = ("dp_0", "dp_1")
TENSOR = ("tensor_0", "tensor_1")
PIPE_TENSOR_DP = ("pipe", "tensor_0", "tensor_1", "dp_0", "dp_1")
TENSOR_DP = ("tensor_0", "tensor_1", "dp_0", "dp_1")


def rows_first(arrays, axis, dims):
    turned = [jnp.moveaxis(a, dim, 0) for a, dim in zip(arrays, dims)]
    both = jnp.concatenate([t.reshape(len(t), -1) for t in turned], axis=1)
    filled, at, done = (lax.all_gather(both, axis, axis=0, tiled=True), 0, [])
    for t, dim in zip(turned, dims):
        section = filled[:, at : at + t[0].size].reshape(-1, *t.shape[1:])
        done.append(jnp.moveaxis(section, 0, dim))
        at += t[0].size
    return tuple(done)


def total_of_pieces(value, axis):
    return lax.all_gather(value, axis).sum(0)


def from_behind(value, axis, by):
    count = lax.axis_size(axis)
    pairs = [(i, i + by) for i in range(count) if 0 <= i + by < count]
    return lax.ppermute(value, axis, pairs)


def by_axis(value, axes):
    for axis in axes:
        value = lax.psum(value, axis)
    return value


def unit_forward(preact, unused):
    return jax.nn.silu(preact).astype(jnp.bfloat16)


def unit_backward(upward, preact):
    sigmoid_value = jax.nn.sigmoid(preact)
    return (upward * sigmoid_value * (1.0 + preact * (1.0 - sigmoid_value))).astype(jnp.bfloat16)


def kahan_add(running, carried, grad_term):
    corrected = grad_term - carried.astype(jnp.float32)
    summed = (running.astype(jnp.float32) + corrected).astype(jnp.bfloat16)
    carried = (summed.astype(jnp.float32) - running.astype(jnp.float32) - corrected).astype(
        jnp.bfloat16
    )
    return (summed, carried)


def contract_last(first_operand, second_operand):
    return lax.dot_general(
        first_operand, second_operand, (((1,), (1,)), ((), ())), preferred_element_type=jnp.float32
    )


def keep_state(state, x_part, act_part, err_part, slope_part):
    return state


def on_device(inputs, w_in, w_out, cotangent):
    sections = lax.axis_size("pipe")
    section_index = lax.axis_index("pipe")
    micro_count = inputs.shape[0]
    step_count = micro_count + sections - 1
    w_first, w_second = rows_first((w_in[0], w_out[0]), DP, (0, 1))
    section_inputs, section_seeds = (inputs, cotangent)
    groups = 1
    stat_rows = section_inputs.shape[1]

    def combine_units(partial_value, unit_fn, kept_stat):
        whole_sum = total_of_pieces(partial_value, TENSOR)
        return (whole_sum, unit_fn(whole_sum, kept_stat))

    row_count = section_inputs.shape[1]
    col_count = section_inputs.shape[2]
    hidden = w_first.shape[1]
    zero_stat = jnp.zeros((stat_rows, hidden), jnp.float32)
    zero_rows = jnp.zeros((row_count, col_count), jnp.bfloat16)
    zero_units = jnp.zeros((row_count, hidden), jnp.float32)

    def project_in(current):
        return jnp.dot(current, w_first, preferred_element_type=jnp.float32)

    def project_back(current):
        return contract_last(current, w_second)

    def no_units(current):
        return zero_units

    def residual_forward(current, activation):
        return (
            current.astype(jnp.float32)
            + jnp.dot(activation, w_second, preferred_element_type=jnp.float32)
        ).astype(jnp.bfloat16)

    def residual_backward(current, slope):
        return (current.astype(jnp.float32) + contract_last(slope, w_first)).astype(jnp.bfloat16)

    def no_rows(current, other):
        return zero_rows

    def forward_step(state_carry, step_index):
        incoming, kept_x, kept_pre, kept_act = state_carry
        micro_index = step_index - section_index
        active = jnp.logical_and(micro_index >= 0, micro_index < micro_count)
        micro_slot = jnp.clip(micro_index, 0, micro_count - 1)
        own_rows = lax.dynamic_index_in_dim(section_inputs, micro_slot, 0, False)
        current = jnp.where(section_index == 0, own_rows, incoming)
        partial_value = lax.cond(active, project_in, no_units, current)
        preact, activation = combine_units(partial_value, unit_forward, zero_stat)
        result = lax.cond(active, residual_forward, no_rows, current, activation)
        kept_x = jnp.where(
            active, lax.dynamic_update_index_in_dim(kept_x, current, micro_slot, 0), kept_x
        )
        kept_pre = jnp.where(
            active, lax.dynamic_update_index_in_dim(kept_pre, preact, micro_slot, 0), kept_pre
        )
        kept_act = jnp.where(
            active, lax.dynamic_update_index_in_dim(kept_act, activation, micro_slot, 0), kept_act
        )
        outgoing = from_behind(result, "pipe", 1)
        return ((outgoing, kept_x, kept_pre, kept_act), None)

    forward_init = (
        zero_rows,
        jnp.zeros((micro_count, row_count, col_count), jnp.bfloat16),
        jnp.zeros((micro_count, stat_rows, hidden), jnp.float32),
        jnp.zeros((micro_count, row_count, hidden), jnp.bfloat16),
    )
    forward_final, unused_out = lax.scan(forward_step, forward_init, jnp.arange(step_count))
    unused_rows, kept_x, kept_pre, kept_act = forward_final

    def accumulate(state, x_part, act_part, err_part, slope_part):
        sum_in, err_in, sum_out, err_out = state
        x_groups = x_part.reshape(groups, -1, col_count)
        slope_groups = slope_part.reshape(groups, -1, hidden)
        act_groups = act_part.reshape(groups, -1, hidden)
        err_groups = err_part.reshape(groups, -1, col_count)
        grad_in = jnp.einsum(
            "gtc,gth->gch", x_groups, slope_groups, preferred_element_type=jnp.float32
        )
        grad_out = jnp.einsum(
            "gth,gtc->ghc", act_groups, err_groups, preferred_element_type=jnp.float32
        )
        sum_in, err_in = kahan_add(sum_in, err_in, grad_in)
        sum_out, err_out = kahan_add(sum_out, err_out, grad_out)
        return (sum_in, err_in, sum_out, err_out)

    def backward_step(state_carry, step_index):
        incoming, sums = state_carry
        micro_index = step_index - (sections - 1 - section_index)
        active = jnp.logical_and(micro_index >= 0, micro_index < micro_count)
        micro_slot = jnp.clip(micro_index, 0, micro_count - 1)
        own_rows = lax.dynamic_index_in_dim(section_seeds, micro_slot, 0, False)
        current = jnp.where(section_index == sections - 1, own_rows, incoming)
        partial_value = lax.cond(active, project_back, no_units, current)
        preact = lax.dynamic_index_in_dim(kept_pre, micro_slot, 0, False)
        unused_stat, slope = combine_units(partial_value, unit_backward, preact)
        x_here = lax.dynamic_index_in_dim(kept_x, micro_slot, 0, False)
        act_here = lax.dynamic_index_in_dim(kept_act, micro_slot, 0, False)
        sums = lax.cond(active, accumulate, keep_state, sums, x_here, act_here, current, slope)
        result = lax.cond(active, residual_backward, no_rows, current, slope)
        outgoing = from_behind(result, "pipe", -1)
        return ((outgoing, sums), None)

    sums_init = (
        jnp.zeros((groups, col_count, hidden), jnp.bfloat16),
        jnp.zeros((groups, col_count, hidden), jnp.bfloat16),
        jnp.zeros((groups, hidden, col_count), jnp.bfloat16),
        jnp.zeros((groups, hidden, col_count), jnp.bfloat16),
    )
    backward_final, unused_back = lax.scan(
        backward_step, (zero_rows, sums_init), jnp.arange(step_count)
    )
    unused_errors, final_sums = backward_final
    sum_in, err_in, sum_out, err_out = final_sums
    total_in = jnp.sum(sum_in.astype(jnp.float32) - err_in.astype(jnp.float32), axis=0)
    total_out = jnp.sum(sum_out.astype(jnp.float32) - err_out.astype(jnp.float32), axis=0)
    total_in, total_out = (
        lax.psum_scatter(total_in, DP, scatter_dimension=0, tiled=True),
        lax.psum_scatter(total_out, DP, scatter_dimension=1, tiled=True),
    )
    squares = jnp.sum(total_in * total_in) + jnp.sum(total_out * total_out)
    norm_squared = by_axis(squares, PIPE_TENSOR_DP)
    grad_norm = jnp.sqrt(norm_squared)
    factor = jnp.minimum(1.0, CLIP_NORM / grad_norm)
    return ((total_in * factor)[None], (total_out * factor)[None], grad_norm)


def solution(mesh):
    split = Mesh(
        mesh.devices.reshape(mesh.shape["pipe"], 2, 2, 4, 4),
        ("pipe", "tensor_0", "tensor_1", "dp_0", "dp_1"),
    )
    placed = (
        P(None, DP, TENSOR),
        P("pipe", TENSOR_DP, None),
        P("pipe", None, TENSOR_DP),
        P(None, DP, TENSOR),
    )
    return jax.shard_map(
        on_device,
        mesh=split,
        in_specs=placed,
        out_specs=(P("pipe", TENSOR_DP, None), P("pipe", None, TENSOR_DP), P()),
        check_vma=False,
    )
```

profile of v0, /device:TPU:0, one launch (start us, length us, event | category | flops | bytes accessed | tf_op | source)
XLA Modules:
  0.0 888.3 jit_solution(17027753523874269229)
XLA Ops:
  10.6 114.0 %all-gather.10.cloned.1.call-done = bf16[4096,2048]{1,0:T(8,128)(2,1)} async-done(((bf16[256,2048]{1,0:T(8,128)(2,1)}), bf16[4096,2048]{1,0:T(8,128)(2,1)}) %all-gather.10.cloned.1.call-update) | async-done | bytes 16777232 | tf_op jit(solution)/shard_map/all_gather | solution.py:17
  124.6 11.7 %fusion.32 = (bf16[4096,1024]{1,0:T(8,128)(2,1)}, bf16[1024,4096]{0,1:T(8,128)(2,1)}) fusion(bf16[4096,2048]{1,0:T(8,128)(2,1)} %all-gather.10.cloned.1.call-done), kind=kLoop, calls=%fused_computation.55 | loop fusion | bytes 33554432 | tf_op jit(solution)/shard_map/slice | solution.py:19
  136.3 11.3 %copy.9 = bf16[1024,4096]{1,0:T(8,128)(2,1)} copy(bf16[1024,4096]{0,1:T(8,128)(2,1)} %get-tuple-element.500) | data formatting | bytes 16777216 | tf_op jit(solution)/shard_map/while | solution.py:181
  150.4 213.6 %while.37 = (s32[]{:T(128)}, bf16[128,4096]{1,0:T(8,128)(2,1)}, bf16[2,128,4096]{2,1,0:T(8,128)(2,1)}, f32[2,128,1024]{2,1,0:T(8,128)S(1)}, bf16[2,128,1024]{2,1...) while((s32[]{:T(128)}, bf16[128,4096]{1,0:T(8,128)(2,1)}, ...), condition=%wide.region_6.7_spmd, body=%wide.region_0.6_spmd.sunk | while | flops 2152071168 | bytes 50332584 | solution.py:139
  160.3 26.3 %all-gather.12.cloned.1.call-done = f32[512,1024]{1,0:T(8,128)} async-done(((f32[128,1024]{1,0:T(8,128)}), f32[512,1024]{1,0:T(8,128)}) %all-gather.12.cloned.1.call-update) | async-done | bytes 2097168 | tf_op jit(solution)/shard_map/while/body/eval_jaxpr/all_gather | solution.py:26
  195.9 23.0 %collective-permute-done = bf16[128,4096]{1,0:T(8,128)(2,1)S(1)} collective-permute-done((bf16[128,4096]{1,0:T(8,128)(2,1)}, bf16[128,4096]{1,0:T(8,128)(2,1)S(1)}, u32[]{:S(2)}, u32[]{:S(2)}) %collective-permute-start) | collective-permute-done | bytes 1048608 | tf_op jit(solution)/shard_map/while/body/eval_jaxpr/ppermute | solution.py:32
  229.8 27.7 %all-gather.12.cloned.1.call-done = f32[512,1024]{1,0:T(8,128)} async-done(((f32[128,1024]{1,0:T(8,128)}), f32[512,1024]{1,0:T(8,128)}) %all-gather.12.cloned.1.call-update) | async-done | bytes 2097168 | tf_op jit(solution)/shard_map/while/body/eval_jaxpr/all_gather | solution.py:26
  267.9 22.8 %collective-permute-done = bf16[128,4096]{1,0:T(8,128)(2,1)S(1)} collective-permute-done((bf16[128,4096]{1,0:T(8,128)(2,1)}, bf16[128,4096]{1,0:T(8,128)(2,1)S(1)}, u32[]{:S(2)}, u32[]{:S(2)}) %collective-permute-start) | collective-permute-done | bytes 1048608 | tf_op jit(solution)/shard_map/while/body/eval_jaxpr/ppermute | solution.py:32
  297.0 32.9 %all-gather.12.cloned.1.call-done = f32[512,1024]{1,0:T(8,128)} async-done(((f32[128,1024]{1,0:T(8,128)}), f32[512,1024]{1,0:T(8,128)}) %all-gather.12.cloned.1.call-update) | async-done | bytes 2097168 | tf_op jit(solution)/shard_map/while/body/eval_jaxpr/all_gather | solution.py:26
  340.3 22.8 %collective-permute-done = bf16[128,4096]{1,0:T(8,128)(2,1)S(1)} collective-permute-done((bf16[128,4096]{1,0:T(8,128)(2,1)}, bf16[128,4096]{1,0:T(8,128)(2,1)S(1)}, u32[]{:S(2)}, u32[]{:S(2)}) %collective-permute-start) | collective-permute-done | bytes 1048608 | tf_op jit(solution)/shard_map/while/body/eval_jaxpr/ppermute | solution.py:32
  381.7 218.9 %while.38 = (s32[]{:T(128)}, bf16[128,4096]{1,0:T(8,128)(2,1)S(1)}, bf16[1,4096,1024]{2,1,0:T(8,128)(2,1)}, bf16[1,4096,1024]{2,1,0:T(8,128)(2,1)}, bf16[1,1024,...) while((s32[]{:T(128)}, bf16[128,4096]{1,0:T(8,128)(2,1)S(1)}, ...), condition=%wide.region_15.16_spmd, body=%wide.region_7.15_spmd.sunk | while | flops 4374134784 | bytes 187172016 | solution.py:181
  385.4 34.3 %all-gather.14.cloned.1.call-done = f32[512,1024]{1,0:T(8,128)} async-done(((f32[128,1024]{1,0:T(8,128)}), f32[512,1024]{1,0:T(8,128)}) %all-gather.14.cloned.1.call-update) | async-done | bytes 2097168 | tf_op jit(solution)/shard_map/while/body/eval_jaxpr/all_gather | solution.py:26
  424.1 30.4 %collective-permute-done.1 = bf16[128,4096]{1,0:T(8,128)(2,1)S(1)} collective-permute-done((bf16[128,4096]{1,0:T(8,128)(2,1)}, bf16[128,4096]{1,0:T(8,128)(2,1)S(1)}, u32[]{:S(2)}, u32[]{:S(2)}) %collective-permute-start.1) | collective-permute-done | bytes 1048608 | tf_op jit(solution)/shard_map/while/body/eval_jaxpr/ppermute | solution.py:32
  464.3 27.5 %all-gather.14.cloned.1.call-done = f32[512,1024]{1,0:T(8,128)} async-done(((f32[128,1024]{1,0:T(8,128)}), f32[512,1024]{1,0:T(8,128)}) %all-gather.14.cloned.1.call-update) | async-done | bytes 2097168 | tf_op jit(solution)/shard_map/while/body/eval_jaxpr/all_gather | solution.py:26
  502.4 25.6 %conditional.14 = ((bf16[1,4096,1024]{2,1,0:T(8,128)(2,1)}, bf16[1,4096,1024]{2,1,0:T(8,128)(2,1)}, bf16[1,1024,4096]{2,1,0:T(8,128)(2,1)}, bf16[1,1024,4096]{2,1,0:T(8,128)(2,1)})) conditional(s32[]{:T(128)} %convert_element_type.173, (bf16[1,4096,1024]{2,1,0:T(8,128)(2,1)}, bf16[1,4096,1024]{2,1,0:T(8,128)(2,1)}, ...), branch_computations={%region_13.13_spmd, %region_14.14_spmd} | conditional | flops 2222981120 | bytes 136839776 | solution.py:170
  502.5 12.9 %fusion.12 = (bf16[1,4096,1024]{2,1,0:T(8,128)(2,1)}, bf16[1,4096,1024]{2,1,0:T(8,128)(2,1)}) fusion(bf16[1,4096,1024]{2,1,0:T(8,128)(2,1)} %get-tuple-element.369, bf16[1,4096,1024]{2,1,0:T(8,128)(2,1)} %get-tuple-element.373, bf16[128,1024]{1,0:T(8,128)(2,1)S(1)} %get-tuple-element.372, bf16[2,128,4096]{2,1,0:T(8,128)(2,1)} %get-tuple-element.370, ...), kind=kOutput, calls=%fused_computation.24 | convolution fusion | flops 1111490560 | bytes 34865664 | tf_op jit(solution)/shard_map/while/body/eval_jaxpr/cond/branch_1_fun/gtc,gth->gch/dot_general | solution.py:148
  538.3 25.6 %all-gather.14.cloned.1.call-done = f32[512,1024]{1,0:T(8,128)} async-done(((f32[128,1024]{1,0:T(8,128)}), f32[512,1024]{1,0:T(8,128)}) %all-gather.14.cloned.1.call-update) | async-done | bytes 2097168 | tf_op jit(solution)/shard_map/while/body/eval_jaxpr/all_gather | solution.py:26
  574.5 25.6 %conditional.14 = ((bf16[1,4096,1024]{2,1,0:T(8,128)(2,1)}, bf16[1,4096,1024]{2,1,0:T(8,128)(2,1)}, bf16[1,1024,4096]{2,1,0:T(8,128)(2,1)}, bf16[1,1024,4096]{2,1,0:T(8,128)(2,1)})) conditional(s32[]{:T(128)} %convert_element_type.173, (bf16[1,4096,1024]{2,1,0:T(8,128)(2,1)}, bf16[1,4096,1024]{2,1,0:T(8,128)(2,1)}, ...), branch_computations={%region_13.13_spmd, %region_14.14_spmd} | conditional | flops 2222981120 | bytes 136839776 | solution.py:170
  574.5 12.9 %fusion.12 = (bf16[1,4096,1024]{2,1,0:T(8,128)(2,1)}, bf16[1,4096,1024]{2,1,0:T(8,128)(2,1)}) fusion(bf16[1,4096,1024]{2,1,0:T(8,128)(2,1)} %get-tuple-element.369, bf16[1,4096,1024]{2,1,0:T(8,128)(2,1)} %get-tuple-element.373, bf16[128,1024]{1,0:T(8,128)(2,1)S(1)} %get-tuple-element.372, bf16[2,128,4096]{2,1,0:T(8,128)(2,1)} %get-tuple-element.370, ...), kind=kOutput, calls=%fused_computation.24 | convolution fusion | flops 1111490560 | bytes 34865664 | tf_op jit(solution)/shard_map/while/body/eval_jaxpr/cond/branch_1_fun/gtc,gth->gch/dot_general | solution.py:148
  600.6 12.2 %subtract_bitcast_fusion = f32[1024,4096]{1,0:T(8,128)} fusion(bf16[1,1024,4096]{2,1,0:T(8,128)(2,1)} %get-tuple-element.414, bf16[1,1024,4096]{2,1,0:T(8,128)(2,1)} %get-tuple-element.413), kind=kLoop, calls=%fused_computation.47 | loop fusion | flops 12582912 | bytes 33554432 | tf_op jit(solution)/shard_map/reduce_sum | solution.py:187
  612.8 13.3 %subtract_bitcast_fusion.1 = f32[4096,1024]{1,0:T(8,128)} fusion(bf16[1,4096,1024]{2,1,0:T(8,128)(2,1)} %get-tuple-element.412, bf16[1,4096,1024]{2,1,0:T(8,128)(2,1)} %get-tuple-element.411), kind=kLoop, calls=%fused_computation.48 | loop fusion | flops 12582912 | bytes 33554432 | tf_op jit(solution)/shard_map/reduce_sum | solution.py:186
  626.1 96.8 %reduce-scatter.5.cloned.1.call-done = f32[1024,256]{1,0:T(8,128)} async-done(((f32[1024,4096]{1,0:T(8,128)}), f32[1024,256]{1,0:T(8,128)}) %reduce-scatter.5.cloned.1.call-update) | async-done | bytes 1048592 | tf_op jit(solution)/shard_map/reduce_scatter | solution.py:190
  725.0 111.5 %reduce-scatter.3.cloned.1.call-done = f32[256,1024]{1,0:T(8,128)} async-done(((f32[4096,1024]{1,0:T(8,128)}), f32[256,1024]{1,0:T(8,128)}) %reduce-scatter.3.cloned.1.call-update) | async-done | bytes 1048592 | tf_op jit(solution)/shard_map/reduce_scatter | solution.py:189
  855.4 10.5 %psum.38 = f32[]{:T(128)} all-reduce(f32[]{:T(128)} %psum.37), channel_id=1, replica_groups=mesh['pipe'=2,'tensor_0'=2,'tensor_1'=2,'dp_0'=4,'dp_1'=4] {'dp_0'}, use_global_device_ids=true, to_apply=%region_23.24 | all-reduce | flops 1 | bytes 8 | tf_op jit(solution)/shard_map/psum | solution.py:37
  (144 shorter events, 233.4 us)
Async XLA Ops:
  7.2 117.4 %all-gather.10.cloned.1.call-start = ((), (), s32[]{:S(2)}) async-start(), calls=%async_computation.2 | async-start | bytes 17825792 | tf_op jit(solution)/shard_map/all_gather | solution.py:17
  150.4 36.2 %all-gather.12.cloned.1.call-start = ((), (), s32[]{:S(2)}) async-start(), calls=%async_computation.5 | async-start | bytes 2621440 | tf_op jit(solution)/shard_map/while/body/eval_jaxpr/all_gather | solution.py:26
  194.3 24.7 %collective-permute-start = (bf16[128,4096]{1,0:T(8,128)(2,1)}, bf16[128,4096]{1,0:T(8,128)(2,1)S(1)}, u32[]{:S(2)}, u32[]{:S(2)}) collective-permute-start(bf16[128,4096]{1,0:T(8,128)(2,1)} %get-tuple-element.782), channel_id=1, source_target_pairs={{0,64},{1,65},{2,66},{3,67},{4,68},{5,69},{6,70},{7,71},{8,72},{9,... | collective-permute-start | bytes 3145736 | tf_op jit(solution)/shard_map/while/body/eval_jaxpr/ppermute | solution.py:32
  219.9 37.6 %all-gather.12.cloned.1.call-start = ((), (), s32[]{:S(2)}) async-start(), calls=%async_computation.5 | async-start | bytes 2621440 | tf_op jit(solution)/shard_map/while/body/eval_jaxpr/all_gather | solution.py:26
  265.1 25.6 %collective-permute-start = (bf16[128,4096]{1,0:T(8,128)(2,1)}, bf16[128,4096]{1,0:T(8,128)(2,1)S(1)}, u32[]{:S(2)}, u32[]{:S(2)}) collective-permute-start(bf16[128,4096]{1,0:T(8,128)(2,1)} %get-tuple-element.782), channel_id=1, source_target_pairs={{0,64},{1,65},{2,66},{3,67},{4,68},{5,69},{6,70},{7,71},{8,72},{9,... | collective-permute-start | bytes 3145736 | tf_op jit(solution)/shard_map/while/body/eval_jaxpr/ppermute | solution.py:32
  291.7 38.2 %all-gather.12.cloned.1.call-start = ((), (), s32[]{:S(2)}) async-start(), calls=%async_computation.5 | async-start | bytes 2621440 | tf_op jit(solution)/shard_map/while/body/eval_jaxpr/all_gather | solution.py:26
  332.9 30.1 %collective-permute-start = (bf16[128,4096]{1,0:T(8,128)(2,1)}, bf16[128,4096]{1,0:T(8,128)(2,1)S(1)}, u32[]{:S(2)}, u32[]{:S(2)}) collective-permute-start(bf16[128,4096]{1,0:T(8,128)(2,1)} %get-tuple-element.782), channel_id=1, source_target_pairs={{0,64},{1,65},{2,66},{3,67},{4,68},{5,69},{6,70},{7,71},{8,72},{9,... | collective-permute-start | bytes 3145736 | tf_op jit(solution)/shard_map/while/body/eval_jaxpr/ppermute | solution.py:32
  364.0 8.8 copy-start.4
  381.8 37.8 %all-gather.14.cloned.1.call-start = ((), (), s32[]{:S(2)}) async-start(), calls=%async_computation.6 | async-start | bytes 2621440 | tf_op jit(solution)/shard_map/while/body/eval_jaxpr/all_gather | solution.py:26
  384.5 37.0 %copy-start.5 = (f32[2,128,1024]{2,1,0:T(8,128)S(1)}, f32[2,128,1024]{2,1,0:T(8,128)}, u32[]{:S(2)}) copy-start(f32[2,128,1024]{2,1,0:T(8,128)} %get-tuple-element.773) | copy-start | bytes 3145732 | tf_op jit(solution)/shard_map/while
  422.8 31.7 %collective-permute-start.1 = (bf16[128,4096]{1,0:T(8,128)(2,1)}, bf16[128,4096]{1,0:T(8,128)(2,1)S(1)}, u32[]{:S(2)}, u32[]{:S(2)}) collective-permute-start(bf16[128,4096]{1,0:T(8,128)(2,1)} %copy-done.7), channel_id=1, source_target_pairs={{64,0},{65,1},{66,2},{67,3},{68,4},{69,5},{70,6},{71,7},{72,8},{73... | collective-permute-start | bytes 3145736 | tf_op jit(solution)/shard_map/while/body/eval_jaxpr/ppermute | solution.py:32
  454.6 37.3 %all-gather.14.cloned.1.call-start = ((), (), s32[]{:S(2)}) async-start(), calls=%async_computation.6 | async-start | bytes 2621440 | tf_op jit(solution)/shard_map/while/body/eval_jaxpr/all_gather | solution.py:26
  457.1 36.5 %copy-start.5 = (f32[2,128,1024]{2,1,0:T(8,128)S(1)}, f32[2,128,1024]{2,1,0:T(8,128)}, u32[]{:S(2)}) copy-start(f32[2,128,1024]{2,1,0:T(8,128)} %get-tuple-element.773) | copy-start | bytes 3145732 | tf_op jit(solution)/shard_map/while
  500.2 1.0 copy-start.7
  501.2 27.4 %collective-permute-start.1 = (bf16[128,4096]{1,0:T(8,128)(2,1)}, bf16[128,4096]{1,0:T(8,128)(2,1)S(1)}, u32[]{:S(2)}, u32[]{:S(2)}) collective-permute-start(bf16[128,4096]{1,0:T(8,128)(2,1)} %copy-done.7), channel_id=1, source_target_pairs={{64,0},{65,1},{66,2},{67,3},{68,4},{69,5},{70,6},{71,7},{72,8},{73... | collective-permute-start | bytes 3145736 | tf_op jit(solution)/shard_map/while/body/eval_jaxpr/ppermute | solution.py:32
  502.5 12.9 %copy-start = (bf16[1,1024,4096]{2,1,0:T(8,128)(2,1)S(1)}, bf16[1,1024,4096]{2,1,0:T(8,128)(2,1)}, u32[]{:S(2)}) copy-start(bf16[1,1024,4096]{2,1,0:T(8,128)(2,1)} %get-tuple-element.374) | copy-start | bytes 25165828 | tf_op jit(solution)/shard_map/while/body/eval_jaxpr/cond
  524.7 3.4 copy-start.1
  528.5 35.4 %all-gather.14.cloned.1.call-start = ((), (), s32[]{:S(2)}) async-start(), calls=%async_computation.6 | async-start | bytes 2621440 | tf_op jit(solution)/shard_map/while/body/eval_jaxpr/all_gather | solution.py:26
  531.1 34.6 %copy-start.5 = (f32[2,128,1024]{2,1,0:T(8,128)S(1)}, f32[2,128,1024]{2,1,0:T(8,128)}, u32[]{:S(2)}) copy-start(f32[2,128,1024]{2,1,0:T(8,128)} %get-tuple-element.773) | copy-start | bytes 3145732 | tf_op jit(solution)/shard_map/while
  573.2 27.4 %collective-permute-start.1 = (bf16[128,4096]{1,0:T(8,128)(2,1)}, bf16[128,4096]{1,0:T(8,128)(2,1)S(1)}, u32[]{:S(2)}, u32[]{:S(2)}) collective-permute-start(bf16[128,4096]{1,0:T(8,128)(2,1)} %copy-done.7), channel_id=1, source_target_pairs={{64,0},{65,1},{66,2},{67,3},{68,4},{69,5},{70,6},{71,7},{72,8},{73... | collective-permute-start | bytes 3145736 | tf_op jit(solution)/shard_map/while/body/eval_jaxpr/ppermute | solution.py:32
  574.5 12.9 %copy-start = (bf16[1,1024,4096]{2,1,0:T(8,128)(2,1)S(1)}, bf16[1,1024,4096]{2,1,0:T(8,128)(2,1)}, u32[]{:S(2)}) copy-start(bf16[1,1024,4096]{2,1,0:T(8,128)(2,1)} %get-tuple-element.374) | copy-start | bytes 25165828 | tf_op jit(solution)/shard_map/while/body/eval_jaxpr/cond
  596.7 3.4 copy-start.1
  600.6 122.3 %reduce-scatter.5.cloned.1.call-start = ((), (), s32[]{:S(2)}) async-start(), calls=%async_computation.4 | async-start | bytes 17825792 | tf_op jit(solution)/shard_map/reduce_scatter | solution.py:190
  612.8 223.7 %reduce-scatter.3.cloned.1.call-start = ((), (), s32[]{:S(2)}) async-start(), calls=%async_computation.3 | async-start | bytes 17825792 | tf_op jit(solution)/shard_map/reduce_scatter | solution.py:189
  (11 other events, 9.6 us)
Sparse Core Ops, SparseCore 0:
  10.7 113.8 all-gather.9
  160.5 26.1 all-gather.11
  229.9 27.5 all-gather.11
  297.1 32.7 all-gather.11
  385.5 34.1 all-gather.13
  464.5 27.3 all-gather.13
  538.4 25.4 all-gather.13
  612.9 109.9 reduce-scatter.4
  726.3 110.0 reduce-scatter.2
where the time goes:
time: 890 us; the launch traced here: 888 us
  waiting for transfers between devices  597 us (67%)
  matrix products  90.1 us (10%)
  local copies, waits for them, and re-layouts  66.9 us (8%)
  other arithmetic  62.4 us (7%)
  blocking collectives  35.5 us (4%)
  between operations  17 us (2%)
  starting transfers between devices  15 us (2%)
    all_gather x6, waiting for transfers between devices, total_of_pieces(): return lax.all_gather(value, axis).sum(0)  174 us
    all_gather x1, waiting for transfers between devices, rows_first(): filled, at, done = (lax.all_gather(both, axis, axis=0, tiled=True), 0, [])  114 us
    reduce_scatter x1, waiting for transfers between devices, on_device(): lax.psum_scatter(total_in, DP, scatter_dimension=0, tiled=True)  111 us
    ppermute x6, waiting for transfers between devices, from_behind(): return lax.ppermute(value, axis, pairs)  100 us
    reduce_scatter x1, waiting for transfers between devices, on_device(): lax.psum_scatter(total_out, DP, scatter_dimension=1, tiled=True)  96.8 us
    psum x5, blocking collectives, by_axis(): value = lax.psum(value, axis)  35.5 us
    dot_general x2, matrix products, accumulate(): jnp.einsum('gtc,gth->gch', x_groups, slope_groups, preferred_element_type...  25.8 us
    dot_general x4, matrix products, contract_last(): lax.dot_general(first_operand, second_operand, (((1,), (1,)), ((), ())),...  25.2 us
  transfers between devices with their start and end apart: 15, of which 15 were waited for; matrix products, arithmetic and copies ran while one was open for 7% of the time, Pallas kernels for 0%

commit v1 on v0

--- a/solution.py
+++ b/solution.py
@@ -11,10 +11,15 @@
 TENSOR_DP = ("tensor_0", "tensor_1", "dp_0", "dp_1")
 
 
+def swapped_in(x, axis, dim):
+    sent = jnp.stack([x] * lax.axis_size(axis))
+    return jnp.concatenate(lax.all_to_all(sent, axis, 0, 0), axis=dim)
+
+
 def rows_first(arrays, axis, dims):
     turned = [jnp.moveaxis(a, dim, 0) for a, dim in zip(arrays, dims)]
     both = jnp.concatenate([t.reshape(len(t), -1) for t in turned], axis=1)
-    filled, at, done = (lax.all_gather(both, axis, axis=0, tiled=True), 0, [])
+    filled, at, done = (swapped_in(both, axis, 0), 0, [])
     for t, dim in zip(turned, dims):
         section = filled[:, at : at + t[0].size].reshape(-1, *t.shape[1:])
         done.append(jnp.moveaxis(section, 0, dim))

time: 890 us -> 1040 us (1.17)
  waiting for transfers between devices: 597 us -> 730 us
    all_to_all x0 -> x1, waiting for transfers between devices: none -> 250 us  [swapped_in(): return jnp.concatenate(lax.all_to_all(sent, axis, 0, 0), axis=dim)]
    all_gather x1 -> x0, waiting for transfers between devices: 114 us -> none  [rows_first(): filled, at, done = (lax.all_gather(both, axis, axis=0, tiled=True), 0, [])]
    another operation x4 -> x5, local copies, waits for them, and re-layouts: 17.5 us -> 23.5 us
  transfers between devices with their start and end apart: 15 -> 15, of which waited for: 15 -> 15; matrix products, arithmetic and copies ran while one was open for 7% -> 6% of each run, Pallas kernels for 0% -> 0%
where the time goes in v1:
time: 1040 us
  waiting for transfers between devices  730 us (70%)
  matrix products  90.1 us (9%)
  local copies, waits for them, and re-layouts  73.7 us (7%)
  other arithmetic  61.5 us (6%)
  blocking collectives  35.5 us (3%)
  starting transfers between devices  23.1 us (2%)
  between operations  18.7 us (2%)
    all_to_all x1, waiting for transfers between devices, swapped_in(): return jnp.concatenate(lax.all_to_all(sent, axis, 0, 0), axis=dim)  250 us
    all_gather x6, waiting for transfers between devices, total_of_pieces(): return lax.all_gather(value, axis).sum(0)  172 us
    reduce_scatter x1, waiting for transfers between devices, on_device(): lax.psum_scatter(total_in, DP, scatter_dimension=0, tiled=True)  111 us
    ppermute x6, waiting for transfers between devices, from_behind(): return lax.ppermute(value, axis, pairs)  100 us
    reduce_scatter x1, waiting for transfers between devices, on_device(): lax.psum_scatter(total_out, DP, scatter_dimension=1, tiled=True)  96.6 us
    psum x5, blocking collectives, by_axis(): value = lax.psum(value, axis)  35.5 us
    dot_general x2, matrix products, accumulate(): jnp.einsum('gtc,gth->gch', x_groups, slope_groups, preferred_element_type...  25.8 us
    dot_general x4, matrix products, contract_last(): lax.dot_general(first_operand, second_operand, (((1,), (1,)), ((), ())),...  25.2 us
  transfers between devices with their start and end apart: 15, of which 15 were waited for; matrix products, arithmetic and copies ran while one was open for 6% of the time, Pallas kernels for 0%

profile of v1, /device:TPU:0, one launch (start us, length us, event | category | flops | bytes accessed | tf_op | source)
XLA Modules:
  0.0 1037.9 jit_solution(12473234596837517246)
XLA Ops:
  25.2 249.9 %all-to-all-done = bf16[16,256,2048]{2,1,0:T(8,128)(2,1)} async-done(((bf16[16,256,2048]{2,1,0:T(8,128)(2,1)}), bf16[16,256,2048]{2,1,0:T(8,128)(2,1)}, u32[]{:S(2)}, u32[]{:S(2)}) %all-to-all-start) | async-done | bytes 16777248 | tf_op jit(solution)/shard_map/all_to_all | solution.py:16
  275.2 11.7 %fusion.32 = (bf16[4096,1024]{1,0:T(8,128)(2,1)}, bf16[1024,4096]{0,1:T(8,128)(2,1)}) fusion(bf16[4096,2048]{1,0:T(8,128)(2,1)} %bitcast.16), kind=kLoop, calls=%fused_computation.55 | loop fusion | bytes 33554432 | tf_op jit(solution)/shard_map/slice | solution.py:24
  286.8 11.6 %copy.10 = bf16[1024,4096]{1,0:T(8,128)(2,1)} copy(bf16[1024,4096]{0,1:T(8,128)(2,1)} %get-tuple-element.500) | data formatting | bytes 16777216 | tf_op jit(solution)/shard_map/while | solution.py:186
  301.2 211.9 %while.37 = (s32[]{:T(128)}, bf16[128,4096]{1,0:T(8,128)(2,1)}, bf16[2,128,4096]{2,1,0:T(8,128)(2,1)}, f32[2,128,1024]{2,1,0:T(8,128)S(1)}, bf16[2,128,1024]{2,1...) while((s32[]{:T(128)}, bf16[128,4096]{1,0:T(8,128)(2,1)}, ...), condition=%wide.region_6.7_spmd, body=%wide.region_0.6_spmd.sunk | while | flops 2152071168 | bytes 50332584 | solution.py:144
  311.2 24.4 %all-gather.9.cloned.1.call-done = f32[512,1024]{1,0:T(8,128)} async-done(((f32[128,1024]{1,0:T(8,128)}), f32[512,1024]{1,0:T(8,128)}) %all-gather.9.cloned.1.call-update) | async-done | bytes 2097168 | tf_op jit(solution)/shard_map/while/body/eval_jaxpr/all_gather | solution.py:31
  344.9 23.0 %collective-permute-done = bf16[128,4096]{1,0:T(8,128)(2,1)S(1)} collective-permute-done((bf16[128,4096]{1,0:T(8,128)(2,1)}, bf16[128,4096]{1,0:T(8,128)(2,1)S(1)}, u32[]{:S(2)}, u32[]{:S(2)}) %collective-permute-start) | collective-permute-done | bytes 1048608 | tf_op jit(solution)/shard_map/while/body/eval_jaxpr/ppermute | solution.py:37
  378.8 27.7 %all-gather.9.cloned.1.call-done = f32[512,1024]{1,0:T(8,128)} async-done(((f32[128,1024]{1,0:T(8,128)}), f32[512,1024]{1,0:T(8,128)}) %all-gather.9.cloned.1.call-update) | async-done | bytes 2097168 | tf_op jit(solution)/shard_map/while/body/eval_jaxpr/all_gather | solution.py:31
  416.9 22.8 %collective-permute-done = bf16[128,4096]{1,0:T(8,128)(2,1)S(1)} collective-permute-done((bf16[128,4096]{1,0:T(8,128)(2,1)}, bf16[128,4096]{1,0:T(8,128)(2,1)S(1)}, u32[]{:S(2)}, u32[]{:S(2)}) %collective-permute-start) | collective-permute-done | bytes 1048608 | tf_op jit(solution)/shard_map/while/body/eval_jaxpr/ppermute | solution.py:37
  446.1 32.9 %all-gather.9.cloned.1.call-done = f32[512,1024]{1,0:T(8,128)} async-done(((f32[128,1024]{1,0:T(8,128)}), f32[512,1024]{1,0:T(8,128)}) %all-gather.9.cloned.1.call-update) | async-done | bytes 2097168 | tf_op jit(solution)/shard_map/while/body/eval_jaxpr/all_gather | solution.py:31
  489.4 22.8 %collective-permute-done = bf16[128,4096]{1,0:T(8,128)(2,1)S(1)} collective-permute-done((bf16[128,4096]{1,0:T(8,128)(2,1)}, bf16[128,4096]{1,0:T(8,128)(2,1)S(1)}, u32[]{:S(2)}, u32[]{:S(2)}) %collective-permute-start) | collective-permute-done | bytes 1048608 | tf_op jit(solution)/shard_map/while/body/eval_jaxpr/ppermute | solution.py:37
  530.7 218.9 %while.38 = (s32[]{:T(128)}, bf16[128,4096]{1,0:T(8,128)(2,1)S(1)}, bf16[1,4096,1024]{2,1,0:T(8,128)(2,1)}, bf16[1,4096,1024]{2,1,0:T(8,128)(2,1)}, bf16[1,1024,...) while((s32[]{:T(128)}, bf16[128,4096]{1,0:T(8,128)(2,1)S(1)}, ...), condition=%wide.region_15.16_spmd, body=%wide.region_7.15_spmd.sunk | while | flops 4374134784 | bytes 187172016 | solution.py:186
  534.5 34.3 %all-gather.11.cloned.1.call-done = f32[512,1024]{1,0:T(8,128)} async-done(((f32[128,1024]{1,0:T(8,128)}), f32[512,1024]{1,0:T(8,128)}) %all-gather.11.cloned.1.call-update) | async-done | bytes 2097168 | tf_op jit(solution)/shard_map/while/body/eval_jaxpr/all_gather | solution.py:31
  573.2 30.4 %collective-permute-done.1 = bf16[128,4096]{1,0:T(8,128)(2,1)S(1)} collective-permute-done((bf16[128,4096]{1,0:T(8,128)(2,1)}, bf16[128,4096]{1,0:T(8,128)(2,1)S(1)}, u32[]{:S(2)}, u32[]{:S(2)}) %collective-permute-start.1) | collective-permute-done | bytes 1048608 | tf_op jit(solution)/shard_map/while/body/eval_jaxpr/ppermute | solution.py:37
  613.4 27.5 %all-gather.11.cloned.1.call-done = f32[512,1024]{1,0:T(8,128)} async-done(((f32[128,1024]{1,0:T(8,128)}), f32[512,1024]{1,0:T(8,128)}) %all-gather.11.cloned.1.call-update) | async-done | bytes 2097168 | tf_op jit(solution)/shard_map/while/body/eval_jaxpr/all_gather | solution.py:31
  651.5 25.6 %conditional.14 = ((bf16[1,4096,1024]{2,1,0:T(8,128)(2,1)}, bf16[1,4096,1024]{2,1,0:T(8,128)(2,1)}, bf16[1,1024,4096]{2,1,0:T(8,128)(2,1)}, bf16[1,1024,4096]{2,1,0:T(8,128)(2,1)})) conditional(s32[]{:T(128)} %convert_element_type.173, (bf16[1,4096,1024]{2,1,0:T(8,128)(2,1)}, bf16[1,4096,1024]{2,1,0:T(8,128)(2,1)}, ...), branch_computations={%region_13.13_spmd, %region_14.14_spmd} | conditional | flops 2222981120 | bytes 136839776 | solution.py:175
  651.5 12.9 %fusion.12 = (bf16[1,4096,1024]{2,1,0:T(8,128)(2,1)}, bf16[1,4096,1024]{2,1,0:T(8,128)(2,1)}) fusion(bf16[1,4096,1024]{2,1,0:T(8,128)(2,1)} %get-tuple-element.369, bf16[1,4096,1024]{2,1,0:T(8,128)(2,1)} %get-tuple-element.373, bf16[128,1024]{1,0:T(8,128)(2,1)S(1)} %get-tuple-element.372, bf16[2,128,4096]{2,1,0:T(8,128)(2,1)} %get-tuple-element.370, ...), kind=kOutput, calls=%fused_computation.24 | convolution fusion | flops 1111490560 | bytes 34865664 | tf_op jit(solution)/shard_map/while/body/eval_jaxpr/cond/branch_1_fun/gtc,gth->gch/dot_general | solution.py:153
  687.4 25.6 %all-gather.11.cloned.1.call-done = f32[512,1024]{1,0:T(8,128)} async-done(((f32[128,1024]{1,0:T(8,128)}), f32[512,1024]{1,0:T(8,128)}) %all-gather.11.cloned.1.call-update) | async-done | bytes 2097168 | tf_op jit(solution)/shard_map/while/body/eval_jaxpr/all_gather | solution.py:31
  723.6 25.6 %conditional.14 = ((bf16[1,4096,1024]{2,1,0:T(8,128)(2,1)}, bf16[1,4096,1024]{2,1,0:T(8,128)(2,1)}, bf16[1,1024,4096]{2,1,0:T(8,128)(2,1)}, bf16[1,1024,4096]{2,1,0:T(8,128)(2,1)})) conditional(s32[]{:T(128)} %convert_element_type.173, (bf16[1,4096,1024]{2,1,0:T(8,128)(2,1)}, bf16[1,4096,1024]{2,1,0:T(8,128)(2,1)}, ...), branch_computations={%region_13.13_spmd, %region_14.14_spmd} | conditional | flops 2222981120 | bytes 136839776 | solution.py:175
  723.6 12.9 %fusion.12 = (bf16[1,4096,1024]{2,1,0:T(8,128)(2,1)}, bf16[1,4096,1024]{2,1,0:T(8,128)(2,1)}) fusion(bf16[1,4096,1024]{2,1,0:T(8,128)(2,1)} %get-tuple-element.369, bf16[1,4096,1024]{2,1,0:T(8,128)(2,1)} %get-tuple-element.373, bf16[128,1024]{1,0:T(8,128)(2,1)S(1)} %get-tuple-element.372, bf16[2,128,4096]{2,1,0:T(8,128)(2,1)} %get-tuple-element.370, ...), kind=kOutput, calls=%fused_computation.24 | convolution fusion | flops 1111490560 | bytes 34865664 | tf_op jit(solution)/shard_map/while/body/eval_jaxpr/cond/branch_1_fun/gtc,gth->gch/dot_general | solution.py:153
  749.6 12.2 %subtract_bitcast_fusion = f32[1024,4096]{1,0:T(8,128)} fusion(bf16[1,1024,4096]{2,1,0:T(8,128)(2,1)} %get-tuple-element.414, bf16[1,1024,4096]{2,1,0:T(8,128)(2,1)} %get-tuple-element.413), kind=kLoop, calls=%fused_computation.47 | loop fusion | flops 12582912 | bytes 33554432 | tf_op jit(solution)/shard_map/reduce_sum | solution.py:192
  761.9 13.3 %subtract_bitcast_fusion.1 = f32[4096,1024]{1,0:T(8,128)} fusion(bf16[1,4096,1024]{2,1,0:T(8,128)(2,1)} %get-tuple-element.412, bf16[1,4096,1024]{2,1,0:T(8,128)(2,1)} %get-tuple-element.411), kind=kLoop, calls=%fused_computation.48 | loop fusion | flops 12582912 | bytes 33554432 | tf_op jit(solution)/shard_map/reduce_sum | solution.py:191
  775.2 96.6 %reduce-scatter.5.cloned.1.call-done = f32[1024,256]{1,0:T(8,128)} async-done(((f32[1024,4096]{1,0:T(8,128)}), f32[1024,256]{1,0:T(8,128)}) %reduce-scatter.5.cloned.1.call-update) | async-done | bytes 1048592 | tf_op jit(solution)/shard_map/reduce_scatter | solution.py:195
  873.9 111.2 %reduce-scatter.3.cloned.1.call-done = f32[256,1024]{1,0:T(8,128)} async-done(((f32[4096,1024]{1,0:T(8,128)}), f32[256,1024]{1,0:T(8,128)}) %reduce-scatter.3.cloned.1.call-update) | async-done | bytes 1048592 | tf_op jit(solution)/shard_map/reduce_scatter | solution.py:194
  1004.1 10.6 %psum.38 = f32[]{:T(128)} all-reduce(f32[]{:T(128)} %psum.37), channel_id=1, replica_groups=mesh['pipe'=2,'tensor_0'=2,'tensor_1'=2,'dp_0'=4,'dp_1'=4] {'dp_0'}, use_global_device_ids=true, to_apply=%region_23.24 | all-reduce | flops 1 | bytes 8 | tf_op jit(solution)/shard_map/psum | solution.py:42
  (145 shorter events, 247.2 us)
Async XLA Ops:
  17.0 258.2 %all-to-all-start = ((bf16[16,256,2048]{2,1,0:T(8,128)(2,1)}), bf16[16,256,2048]{2,1,0:T(8,128)(2,1)}, u32[]{:S(2)}, u32[]{:S(2)}) async-start(bf16[16,256,2048]{2,1,0:T(8,128)(2,1)} %stack.2), calls=%async_computation | async-start | bytes 33554432 | tf_op jit(solution)/shard_map/all_to_all | solution.py:16
  301.2 34.4 %all-gather.9.cloned.1.call-start = ((), (), s32[]{:S(2)}) async-start(), calls=%async_computation.5 | async-start | bytes 2621440 | tf_op jit(solution)/shard_map/while/body/eval_jaxpr/all_gather | solution.py:31
  343.2 24.7 %collective-permute-start = (bf16[128,4096]{1,0:T(8,128)(2,1)}, bf16[128,4096]{1,0:T(8,128)(2,1)S(1)}, u32[]{:S(2)}, u32[]{:S(2)}) collective-permute-start(bf16[128,4096]{1,0:T(8,128)(2,1)} %get-tuple-element.782), channel_id=1, source_target_pairs={{0,64},{1,65},{2,66},{3,67},{4,68},{5,69},{6,70},{7,71},{8,72},{9,... | collective-permute-start | bytes 3145736 | tf_op jit(solution)/shard_map/while/body/eval_jaxpr/ppermute | solution.py:37
  368.9 37.6 %all-gather.9.cloned.1.call-start = ((), (), s32[]{:S(2)}) async-start(), calls=%async_computation.5 | async-start | bytes 2621440 | tf_op jit(solution)/shard_map/while/body/eval_jaxpr/all_gather | solution.py:31
  414.1 25.6 %collective-permute-start = (bf16[128,4096]{1,0:T(8,128)(2,1)}, bf16[128,4096]{1,0:T(8,128)(2,1)S(1)}, u32[]{:S(2)}, u32[]{:S(2)}) collective-permute-start(bf16[128,4096]{1,0:T(8,128)(2,1)} %get-tuple-element.782), channel_id=1, source_target_pairs={{0,64},{1,65},{2,66},{3,67},{4,68},{5,69},{6,70},{7,71},{8,72},{9,... | collective-permute-start | bytes 3145736 | tf_op jit(solution)/shard_map/while/body/eval_jaxpr/ppermute | solution.py:37
  440.7 38.3 %all-gather.9.cloned.1.call-start = ((), (), s32[]{:S(2)}) async-start(), calls=%async_computation.5 | async-start | bytes 2621440 | tf_op jit(solution)/shard_map/while/body/eval_jaxpr/all_gather | solution.py:31
  482.0 30.1 %collective-permute-start = (bf16[128,4096]{1,0:T(8,128)(2,1)}, bf16[128,4096]{1,0:T(8,128)(2,1)S(1)}, u32[]{:S(2)}, u32[]{:S(2)}) collective-permute-start(bf16[128,4096]{1,0:T(8,128)(2,1)} %get-tuple-element.782), channel_id=1, source_target_pairs={{0,64},{1,65},{2,66},{3,67},{4,68},{5,69},{6,70},{7,71},{8,72},{9,... | collective-permute-start | bytes 3145736 | tf_op jit(solution)/shard_map/while/body/eval_jaxpr/ppermute | solution.py:37
  513.1 8.8 copy-start.4
  530.9 37.8 %all-gather.11.cloned.1.call-start = ((), (), s32[]{:S(2)}) async-start(), calls=%async_computation.6 | async-start | bytes 2621440 | tf_op jit(solution)/shard_map/while/body/eval_jaxpr/all_gather | solution.py:31
  533.6 37.0 %copy-start.5 = (f32[2,128,1024]{2,1,0:T(8,128)S(1)}, f32[2,128,1024]{2,1,0:T(8,128)}, u32[]{:S(2)}) copy-start(f32[2,128,1024]{2,1,0:T(8,128)} %get-tuple-element.773) | copy-start | bytes 3145732 | tf_op jit(solution)/shard_map/while
  570.9 1.0 copy-start.7
  571.9 31.7 %collective-permute-start.1 = (bf16[128,4096]{1,0:T(8,128)(2,1)}, bf16[128,4096]{1,0:T(8,128)(2,1)S(1)}, u32[]{:S(2)}, u32[]{:S(2)}) collective-permute-start(bf16[128,4096]{1,0:T(8,128)(2,1)} %copy-done.7), channel_id=1, source_target_pairs={{64,0},{65,1},{66,2},{67,3},{68,4},{69,5},{70,6},{71,7},{72,8},{73... | collective-permute-start | bytes 3145736 | tf_op jit(solution)/shard_map/while/body/eval_jaxpr/ppermute | solution.py:37
  603.6 37.3 %all-gather.11.cloned.1.call-start = ((), (), s32[]{:S(2)}) async-start(), calls=%async_computation.6 | async-start | bytes 2621440 | tf_op jit(solution)/shard_map/while/body/eval_jaxpr/all_gather | solution.py:31
  606.2 36.5 %copy-start.5 = (f32[2,128,1024]{2,1,0:T(8,128)S(1)}, f32[2,128,1024]{2,1,0:T(8,128)}, u32[]{:S(2)}) copy-start(f32[2,128,1024]{2,1,0:T(8,128)} %get-tuple-element.773) | copy-start | bytes 3145732 | tf_op jit(solution)/shard_map/while
  650.2 27.4 %collective-permute-start.1 = (bf16[128,4096]{1,0:T(8,128)(2,1)}, bf16[128,4096]{1,0:T(8,128)(2,1)S(1)}, u32[]{:S(2)}, u32[]{:S(2)}) collective-permute-start(bf16[128,4096]{1,0:T(8,128)(2,1)} %copy-done.7), channel_id=1, source_target_pairs={{64,0},{65,1},{66,2},{67,3},{68,4},{69,5},{70,6},{71,7},{72,8},{73... | collective-permute-start | bytes 3145736 | tf_op jit(solution)/shard_map/while/body/eval_jaxpr/ppermute | solution.py:37
  651.5 12.9 %copy-start = (bf16[1,1024,4096]{2,1,0:T(8,128)(2,1)S(1)}, bf16[1,1024,4096]{2,1,0:T(8,128)(2,1)}, u32[]{:S(2)}) copy-start(bf16[1,1024,4096]{2,1,0:T(8,128)(2,1)} %get-tuple-element.374) | copy-start | bytes 25165828 | tf_op jit(solution)/shard_map/while/body/eval_jaxpr/cond
  673.7 3.3 copy-start.1
  677.6 35.4 %all-gather.11.cloned.1.call-start = ((), (), s32[]{:S(2)}) async-start(), calls=%async_computation.6 | async-start | bytes 2621440 | tf_op jit(solution)/shard_map/while/body/eval_jaxpr/all_gather | solution.py:31
  680.2 34.6 %copy-start.5 = (f32[2,128,1024]{2,1,0:T(8,128)S(1)}, f32[2,128,1024]{2,1,0:T(8,128)}, u32[]{:S(2)}) copy-start(f32[2,128,1024]{2,1,0:T(8,128)} %get-tuple-element.773) | copy-start | bytes 3145732 | tf_op jit(solution)/shard_map/while
  722.3 27.4 %collective-permute-start.1 = (bf16[128,4096]{1,0:T(8,128)(2,1)}, bf16[128,4096]{1,0:T(8,128)(2,1)S(1)}, u32[]{:S(2)}, u32[]{:S(2)}) collective-permute-start(bf16[128,4096]{1,0:T(8,128)(2,1)} %copy-done.7), channel_id=1, source_target_pairs={{64,0},{65,1},{66,2},{67,3},{68,4},{69,5},{70,6},{71,7},{72,8},{73... | collective-permute-start | bytes 3145736 | tf_op jit(solution)/shard_map/while/body/eval_jaxpr/ppermute | solution.py:37
  723.6 12.9 %copy-start = (bf16[1,1024,4096]{2,1,0:T(8,128)(2,1)S(1)}, bf16[1,1024,4096]{2,1,0:T(8,128)(2,1)}, u32[]{:S(2)}) copy-start(bf16[1,1024,4096]{2,1,0:T(8,128)(2,1)} %get-tuple-element.374) | copy-start | bytes 25165828 | tf_op jit(solution)/shard_map/while/body/eval_jaxpr/cond
  745.8 3.3 copy-start.1
  749.6 122.1 %reduce-scatter.5.cloned.1.call-start = ((), (), s32[]{:S(2)}) async-start(), calls=%async_computation.4 | async-start | bytes 17825792 | tf_op jit(solution)/shard_map/reduce_scatter | solution.py:195
  761.8 223.3 %reduce-scatter.3.cloned.1.call-start = ((), (), s32[]{:S(2)}) async-start(), calls=%async_computation.3 | async-start | bytes 17825792 | tf_op jit(solution)/shard_map/reduce_scatter | solution.py:194
  (11 other events, 9.6 us)
Sparse Core Ops, SparseCore 0:
  311.3 24.2 all-gather.8
  379.0 27.5 all-gather.8
  446.2 32.7 all-gather.8
  534.6 34.1 all-gather.10
  613.5 27.3 all-gather.10
  687.5 25.4 all-gather.10
Sparse Core Ops, SparseCore 1:
  761.9 109.8 reduce-scatter.4
  875.1 110.0 reduce-scatter.2
